TPU v7x, 32 devices: a whole 2x2x4 slice. The times are simulated.
32 devices in a mesh: samp: 8 (over z, y), snp: 4 (over x, core).
Axes of the slice: x: 2, y: 2, z: 4, core: 2. Of those that a mesh axis runs over, the one named last changes fastest.
Arguments:
- geno_words: int32 [2048, 1024], P('samp', 'snp'), may hold values from -2147483648 to 2147483647, as said below
- counts: int32 [2048], P('samp'), may hold values from 0 to 4, as said below
- probes: bfloat16 [2048, 64], P('samp'), may hold values from -6 to 6
- phenotype: float32 [2048], P('samp'), may hold values from -6 to 6
- tile_comp: int32 [128], replicated, may hold values from 0 to 7, as said below
Outputs:
- images: bfloat16 [2048, 512], P(('samp', 'snp'))
- traces: float32 [8, 8], replicated
- yky: float32 [8], replicated
Inputs may be any that keep to these rules, and one draw needn't show every extreme that they name: `geno_words`: each word packs sixteen dosages of one sample in 2-bit fields as step one reads them; every field holds 0, 1 or 2. `counts`: at least one sample has a count of one or more. `tile_comp`: every component owns at least one tile.
All inputs are finite; a program needn't handle non-finite values.
Results may differ from a plain program's by a relative error of at most 0.015.
Values may be sent and summed in bfloat16 or wider, within the bound.
A program may use at most 64 MiB of HBM per device.

v0:
```python
import jax
import jax.numpy as jnp
from jax import lax
from jax.sharding import PartitionSpec as P

SNPS = 16384
COMPS = 8
EPSILON = 1e-05


def unpack_rows(packed):
    height = packed.shape[0]
    grouped = packed.reshape(height, -1, 1, 128)
    shifts = 2 * jnp.arange(16, dtype=jnp.int32).reshape(1, 1, 16, 1)
    fields = jnp.right_shift(grouped, shifts) & 3
    return fields.reshape(height, -1).astype(jnp.bfloat16)


def block_number(row_count):
    number = 1
    while row_count // number > 768 or row_count % number != 0:
        number = number + 1
    return number


def finish(panel_part, moment_part, totals, inverse, member):
    weight_total = totals[0]
    pheno_total = totals[1]
    probe_total = totals[2:]
    average = moment_part[0] / weight_total
    second = moment_part[1] / weight_total
    spread = 1.0 / jnp.sqrt(second - average * average + EPSILON)
    unit_panel = spread[:, None] * (panel_part - average[:, None] * probe_total[None, :])
    pheno_unit = spread * (moment_part[2] - average * pheno_total)
    coefficients = (spread[:, None] * unit_panel * inverse[:, None]).astype(jnp.bfloat16)
    energy = jnp.sum(member * (pheno_unit * pheno_unit * inverse)[:, None], axis=0)
    return (average, coefficients, energy)


def on_device(geno_words, counts, probes, phenotype, tile_comp):
    height = geno_words.shape[0]
    snp_local = geno_words.shape[1] * 16
    tile_local = snp_local // 128
    probe_count = probes.shape[1]
    weights = counts.astype(jnp.float32)
    root_weight = jnp.sqrt(weights)
    probe_rows = (probes.astype(jnp.float32) * root_weight[:, None]).astype(jnp.bfloat16)
    pheno_rows = (phenotype * root_weight).astype(jnp.bfloat16)
    count_rows = counts.astype(jnp.bfloat16)
    left_rows = jnp.stack([count_rows, pheno_rows], axis=1)
    dosage = unpack_rows(geno_words)
    cross_panel = jnp.einsum("rj,rb->jb", dosage, probe_rows, preferred_element_type=jnp.float32)
    linear = jnp.einsum("rc,rj->cj", left_rows, dosage, preferred_element_type=jnp.float32)
    squares = jnp.einsum("r,rj->j", count_rows, dosage * dosage, preferred_element_type=jnp.float32)
    moments = jnp.stack([linear[0], squares, linear[1]])
    totals = jnp.concatenate(
        [
            jnp.sum(weights)[None],
            jnp.sum(pheno_rows.astype(jnp.float32))[None],
            jnp.sum(probe_rows.astype(jnp.float32), axis=0),
        ]
    )
    levels = jnp.arange(COMPS, dtype=jnp.int32)
    member_all = (tile_comp[:, None] == levels[None, :]).astype(jnp.float32)
    comp_sizes = 128.0 * jnp.sum(member_all, axis=0)
    member_tiles = lax.dynamic_slice_in_dim(
        member_all, lax.axis_index("snp") * tile_local, tile_local, 0
    )
    member_snps = jnp.repeat(member_tiles, 128, axis=0)
    inverse = jnp.sum(member_snps * (1.0 / comp_sizes)[None, :], axis=1)
    summed_panel, summed_moments, totals = lax.psum(
        (cross_panel.reshape(-1, 128), moments, totals), "samp"
    )
    average, coefficients, energy = finish(
        summed_panel.reshape(snp_local, probe_count), summed_moments, totals, inverse, member_snps
    )
    energy = lax.psum(energy, "snp")
    coef_tiles = coefficients.reshape(tile_local, 128, probe_count)
    centre = jnp.sum(average.reshape(tile_local, 128, 1) * coef_tiles.astype(jnp.float32), axis=1)
    quarter = height // lax.axis_size("snp")
    inner_count = block_number(quarter * lax.axis_size("snp"))
    piece_rows = quarter * lax.axis_size("snp") // inner_count
    dosage = unpack_rows(geno_words)
    dosage = dosage.reshape(piece_rows, tile_local, 128)
    partial_value = (
        jnp.einsum("rtj,tjb->rtb", dosage, coef_tiles, preferred_element_type=jnp.float32)
        - centre[None]
    )
    grouped = jnp.einsum(
        "rtb,tk->rkb", partial_value, member_tiles, precision=lax.Precision.HIGHEST
    )
    scaled = grouped * root_weight[:, None, None]
    pieces = scaled.reshape(piece_rows, COMPS * probe_count)
    own_images = lax.psum_scatter(pieces, "snp", scatter_dimension=0, tiled=True)
    stacked = own_images.reshape(quarter, COMPS, probe_count)
    local_trace = jnp.einsum("rkb,rlb->kl", stacked, stacked, precision=lax.Precision.HIGHEST)
    trace_sum = lax.psum(local_trace, ("samp", "snp"))
    weight_total = totals[0]
    traces = trace_sum * (SNPS / (COMPS * probe_count)) / (weight_total * weight_total)
    return (own_images.astype(jnp.bfloat16), traces, energy / weight_total)


def solution(mesh):
    in_specs = (P("samp", "snp"), P("samp"), P("samp", None), P("samp"), P())
    out_specs = (P(("samp", "snp"), None), P(), P())
    return jax.shard_map(
        on_device, mesh=mesh, in_specs=in_specs, out_specs=out_specs, check_vma=False
    )
```

profile of v0, /device:TPU:0, one launch (start us, length us, event | category | flops | bytes accessed | tf_op | source)
XLA Modules:
  0.0 172.9 jit_solution(4429881836668498962)
XLA Ops:
  7.2 0.0 copy-start
  7.2 0.0 all-reduce.3.cloned.1.call-start
  7.2 1.1 copy.42
  8.3 1.3 convert_reduce_fusion.2
  9.6 0.1 shift_right_arithmetic.43
  9.7 0.7 fusion.1
  10.4 0.0 copy-done
  10.4 0.7 convolution_bitcast_fusion
  11.2 0.0 copy-start.1
  11.2 0.0 copy-start.2
  11.2 1.1 copy.55
  12.3 0.0 all-reduce.3.cloned.1.call-update
  12.3 0.0 reduce-scatter.4.cloned.1.call-start
  12.4 0.0 copy-done.1
  12.4 0.1 convert_reduce_fusion
  12.5 0.0 copy-done.2
  12.5 0.1 convert_reduce_fusion.1
  12.7 0.6 fusion.7
  13.3 0.7 fusion.18
  14.0 1.4 pad_maximum_fusion.1
  15.4 40.4 %all-reduce = (f32[66]{0:T(128)S(1)}, f32[3,4096]{1,0:T(4,128)S(1)}) all-reduce(f32[66]{0:T(128)S(1)} %pad_maximum_fusion.1, f32[3,4096]{1,0:T(4,128)S(1)} %pad_maximum_fusion), channel_id=1, replica_groups=mesh['samp'=8,'snp'=4] {'samp'}, use_global_device_ids=true, to_apply=%region_4.0 | all-reduce | flops 12354 | bytes 98832 | tf_op jit(solution)/shard_map/psum | solution.py:71
  55.9 0.1 slice.30
  55.9 0.6 fusion.28
  56.5 0.1 shift_right_arithmetic.49
  56.6 0.1 constant_dynamic-slice_fusion
  56.7 0.1 copy.35
  56.8 2.5 %shift_right_arithmetic.41 = s32[256,2,16,128]{0,3,2,1:T(8,128)} broadcast(s32[256,2,128]{0,2,1:T(8,128)S(1)} %bitcast.41), dimensions={0,1,3} | broadcast | bytes 4456448 | tf_op jit(solution)/shard_map/shift_right_arithmetic | solution.py:15
  59.2 5.6 %copy.36 = s32[256,32,128]{2,0,1:T(8,128)} copy(s32[256,32,128]{0,2,1:T(8,128)} %bitcast.38) | data formatting | bytes 8388608 | tf_op jit(solution)/shard_map/shift_right_arithmetic | solution.py:15
  64.8 0.1 multiply_reduce_fusion.2
  64.9 0.7 fusion.26
  65.6 0.7 multiply_multiply_fusion
  66.3 28.1 %all-reduce.3.cloned.1.call-done = f32[32,128,64]{1,2,0:T(8,128)} async-done(((f32[32,128,64]{1,2,0:T(8,128)}), f32[32,128,64]{1,2,0:T(8,128)}) %all-reduce.3.cloned.1.call-update) | async-done | bytes 1048592 | tf_op jit(solution)/shard_map/psum | solution.py:71
  94.4 1.7 multiply_reduce_fusion
  96.0 3.1 %subtract_bitcast_fusion = f32[256,32,64]{0,2,1:T(8,128)S(1)} fusion(bf16[32,128,64]{1,2,0:T(8,128)(2,1)S(1)} %get-tuple-element.18, s32[256,32,128]{2,0,1:T(8,128)} %copy.36, s32[32]{0:T(128)S(1)} %shift_right_arithmetic.49, f32[32,64]{1,0:T(8,128)S(1)} %get-tuple-element.17), kind=kOutput, calls=%fused_computation.7 | convolution fusion | flops 137887744 | bytes 6824064 | tf_op jit(solution)/shard_map/rtj,tjb->rtb/dot_general | solution.py:86
  99.1 2.0 %fusion.12 = f32[256,8,64]{0,1,2:T(8,128)S(1)} fusion(f32[256,32,64]{0,2,1:T(8,128)S(1)} %subtract_bitcast_fusion, f32[256]{0:T(256)S(1)} %get-tuple-element.29, pred[128,8]{0,1:T(8,128)(4,1)S(1)} %get-tuple-element.32, s32[]{:T(128)S(6)} %select_n.3), kind=kOutput, calls=%fused_computation.14 | convolution fusion | flops 50462720 | bytes 2623492 | tf_op jit(solution)/shard_map/rtb,tk->rkb/dot_general | solution.py:89
  101.1 0.2 copy.38
  101.3 1.0 copy.43
  102.3 0.0 reduce-scatter.4.cloned.1.call-update
  102.3 0.2 multiply_reduce_fusion.1
  102.5 6.5 %psum.39 = f32[8]{0:T(128)S(1)} all-reduce(f32[8]{0:T(128)S(1)} %multiply_reduce_fusion.1), channel_id=1, replica_groups=mesh['samp'=8,'snp'=4] {'snp'}, use_global_device_ids=true, to_apply=%region_12.0 | all-reduce | flops 8 | bytes 64 | tf_op jit(solution)/shard_map/psum | solution.py:77
  110.3 1.2 broadcast_divide_fusion
  111.5 12.2 %reduce-scatter.4.cloned.1.call-done = f32[64,512]{1,0:T(8,128)} async-done(((f32[256,512]{1,0:T(8,128)}), f32[64,512]{1,0:T(8,128)}) %reduce-scatter.4.cloned.1.call-update) | async-done | bytes 131088
  123.7 1.0 copy.44
  124.7 0.7 convolution_bitcast_fusion.1
  125.5 39.3 %psum.38 = f32[8,8]{1,0:T(8,128)S(1)} all-reduce(f32[8,8]{1,0:T(8,128)S(1)} %convolution_bitcast_fusion.1), channel_id=1, replica_groups=mesh['samp'=8,'snp'=4] {'samp','snp'}, use_global_device_ids=true, to_apply=%region_10.0 | all-reduce | flops 64 | bytes 512 | tf_op jit(solution)/shard_map/psum | solution.py:97
  164.8 0.7 copy.41
  165.5 0.6 multiply_divide_fusion
  (10 shorter events, 0.1 us)
Async XLA Ops:
  7.2 3.3 %copy-start = (bf16[256,64]{0,1:T(8,128)(2,1)S(1)}, bf16[256,64]{0,1:T(8,128)(2,1)}, u32[]{:S(2)}) copy-start(bf16[256,64]{0,1:T(8,128)(2,1)} %param.7) | copy-start | bytes 98308
  7.2 87.2 %all-reduce.3.cloned.1.call-start = ((), (), s32[]{:S(2)}) async-start(), calls=%async_computation.1 | async-start | bytes 2097152 | tf_op jit(solution)/shard_map/psum | solution.py:71
  11.2 1.2 copy-start.1
  11.2 1.3 copy-start.2
  12.3 111.4 %reduce-scatter.4.cloned.1.call-start = ((), (), s32[]{:S(2)}) async-start(), calls=%async_computation.2 | async-start | bytes 655360
Sparse Core Ops, SparseCore 0:
  12.4 81.8 all-reduce.2
  102.4 21.2 reduce-scatter.3
where the time goes:
time: 173 us
  blocking collectives  86.2 us (50%)
  waiting for transfers between devices  40.3 us (23%)
  between operations  15.5 us (9%)
  local copies, waits for them, and re-layouts  14.2 us (8%)
  other arithmetic  8.78 us (5%)
  matrix products  7.85 us (5%)
    psum x1, blocking collectives, on_device(): lax.psum((cross_panel.reshape(-1, 128), moments, totals), 'samp')  40.4 us
    psum x1, blocking collectives, on_device(): trace_sum = lax.psum(local_trace, ('samp', 'snp'))  39.3 us
    psum x1, waiting for transfers between devices, on_device(): lax.psum((cross_panel.reshape(-1, 128), moments, totals), 'samp')  28.1 us
    unnamed x3, waiting for transfers between devices  12.2 us
    shift_right_arithmetic x6, local copies, waits for them, and re-layouts, unpack_rows(): fields = jnp.right_shift(grouped, shifts) & 3  9.3 us
    psum x1, blocking collectives, on_device(): energy = lax.psum(energy, 'snp')  6.51 us
  transfers between devices with their start and end apart: 2, of which 2 were waited for; matrix products, arithmetic and copies ran while one was open for 9% of the time, Pallas kernels for 0%

commit v1 on v0

--- a/solution.py
+++ b/solution.py
@@ -94,7 +94,7 @@
     own_images = lax.psum_scatter(pieces, "snp", scatter_dimension=0, tiled=True)
     stacked = own_images.reshape(quarter, COMPS, probe_count)
     local_trace = jnp.einsum("rkb,rlb->kl", stacked, stacked, precision=lax.Precision.HIGHEST)
-    trace_sum = lax.psum(local_trace, ("samp", "snp"))
+    trace_sum = jax.lax.psum(jax.lax.psum(local_trace, axis_name="snp"), axis_name="samp")
     weight_total = totals[0]
     traces = trace_sum * (SNPS / (COMPS * probe_count)) / (weight_total * weight_total)
     return (own_images.astype(jnp.bfloat16), traces, energy / weight_total)

time: 173 us -> 163 us (0.942)
  blocking collectives: 86.2 us -> 67.9 us
  waiting for transfers between devices: 40.3 us -> 48 us
    psum x2, blocking collectives: 45.8 us -> 27.5 us  [the longest x1 21.6 us: on_device(): jax.lax.psum(jax.lax.psum(local_trace, axis_name='snp'), axis_name='samp')]
    unnamed x3, waiting for transfers between devices: 12.2 us -> 19.9 us
  transfers between devices with their start and end apart: 2 -> 2, of which waited for: 2 -> 2; matrix products, arithmetic and copies ran while one was open for 9% -> 8% of each run, Pallas kernels for 0% -> 0%
where the time goes in v1:
time: 163 us; the launch traced here: 162 us
  blocking collectives  67.9 us (42%)
  waiting for transfers between devices  48 us (29%)
  between operations  15.5 us (10%)
  local copies, waits for them, and re-layouts  14.2 us (9%)
  other arithmetic  8.77 us (5%)
  matrix products  7.85 us (5%)
    psum x1, blocking collectives, on_device(): lax.psum((cross_panel.reshape(-1, 128), moments, totals), 'samp')  40.4 us
    psum x1, waiting for transfers between devices, on_device(): lax.psum((cross_panel.reshape(-1, 128), moments, totals), 'samp')  28.1 us
    psum x1, blocking collectives, on_device(): jax.lax.psum(jax.lax.psum(local_trace, axis_name='snp'), axis_name='samp')  21.6 us
    unnamed x3, waiting for transfers between devices  19.9 us
    shift_right_arithmetic x6, local copies, waits for them, and re-layouts, unpack_rows(): fields = jnp.right_shift(grouped, shifts) & 3  9.3 us
    psum x1, blocking collectives, on_device(): jax.lax.psum(local_trace, axis_name='snp')  5.85 us
  transfers between devices with their start and end apart: 2, of which 2 were waited for; matrix products, arithmetic and copies ran while one was open for 8% of the time, Pallas kernels for 0%

profile of v1, /device:TPU:0, one launch (start us, length us, event | category | flops | bytes accessed | tf_op | source)
XLA Modules:
  0.0 162.3 jit_solution(14717312680185877962)
XLA Ops:
  7.2 0.0 copy-start
  7.2 0.0 all-reduce.4.cloned.1.call-start
  7.2 1.1 copy.42
  8.3 1.3 convert_reduce_fusion.2
  9.6 0.1 shift_right_arithmetic.43
  9.7 0.7 fusion.1
  10.4 0.0 copy-done
  10.4 0.7 convolution_bitcast_fusion
  11.2 0.0 copy-start.1
  11.2 0.0 copy-start.2
  11.2 1.1 copy.55
  12.3 0.0 all-reduce.4.cloned.1.call-update
  12.3 0.0 reduce-scatter.4.cloned.1.call-start
  12.4 0.0 copy-done.1
  12.4 0.1 convert_reduce_fusion
  12.5 0.0 copy-done.2
  12.5 0.1 convert_reduce_fusion.1
  12.7 0.6 fusion.7
  13.3 0.7 fusion.18
  14.0 1.4 pad_maximum_fusion.1
  15.4 40.4 %all-reduce = (f32[66]{0:T(128)S(1)}, f32[3,4096]{1,0:T(4,128)S(1)}) all-reduce(f32[66]{0:T(128)S(1)} %pad_maximum_fusion.1, f32[3,4096]{1,0:T(4,128)S(1)} %pad_maximum_fusion), channel_id=1, replica_groups=mesh['samp'=8,'snp'=4] {'samp'}, use_global_device_ids=true, to_apply=%region_4.0 | all-reduce | flops 12354 | bytes 98832 | tf_op jit(solution)/shard_map/psum | solution.py:71
  55.9 0.1 slice.30
  55.9 0.6 fusion.28
  56.5 0.1 shift_right_arithmetic.49
  56.6 0.1 constant_dynamic-slice_fusion
  56.7 0.1 copy.35
  56.8 2.5 %shift_right_arithmetic.41 = s32[256,2,16,128]{0,3,2,1:T(8,128)} broadcast(s32[256,2,128]{0,2,1:T(8,128)S(1)} %bitcast.41), dimensions={0,1,3} | broadcast | bytes 4456448 | tf_op jit(solution)/shard_map/shift_right_arithmetic | solution.py:15
  59.2 5.6 %copy.36 = s32[256,32,128]{2,0,1:T(8,128)} copy(s32[256,32,128]{0,2,1:T(8,128)} %bitcast.38) | data formatting | bytes 8388608 | tf_op jit(solution)/shard_map/shift_right_arithmetic | solution.py:15
  64.8 0.1 multiply_reduce_fusion.2
  64.9 0.7 fusion.26
  65.6 0.7 multiply_multiply_fusion
  66.3 28.1 %all-reduce.4.cloned.1.call-done = f32[32,128,64]{1,2,0:T(8,128)} async-done(((f32[32,128,64]{1,2,0:T(8,128)}), f32[32,128,64]{1,2,0:T(8,128)}) %all-reduce.4.cloned.1.call-update) | async-done | bytes 1048592 | tf_op jit(solution)/shard_map/psum | solution.py:71
  94.4 1.7 %multiply_reduce_fusion = (f32[32,64]{1,0:T(8,128)S(1)}, bf16[32,128,64]{1,2,0:T(8,128)(2,1)S(1)}) fusion(f32[32,128]{1,0:T(8,128)S(1)} %bitcast.45, f32[32,128]{1,0:T(8,128)S(1)} %multiply_reduce_fusion.2, f32[32,128,64]{1,2,0:T(8,128)} %all-reduce.4.cloned.1.call-done, f32[64]{0:T(128)S(1)} %slice.30, f32[32,128]{1,0:T(8,128)S(1)} %get-tuple-element.27), kind=kLoop, calls=%fused_computation.17 | loop fusion | flops 2357248 | bytes 1630464 | tf_op jit(solution)/shard_map/reduce_sum | solution.py:79
  96.0 3.1 %subtract_bitcast_fusion = f32[256,32,64]{0,2,1:T(8,128)S(1)} fusion(bf16[32,128,64]{1,2,0:T(8,128)(2,1)S(1)} %get-tuple-element.20, s32[256,32,128]{2,0,1:T(8,128)} %copy.36, s32[32]{0:T(128)S(1)} %shift_right_arithmetic.49, f32[32,64]{1,0:T(8,128)S(1)} %get-tuple-element.19), kind=kOutput, calls=%fused_computation.7 | convolution fusion | flops 137887744 | bytes 6824064 | tf_op jit(solution)/shard_map/rtj,tjb->rtb/dot_general | solution.py:86
  99.1 2.0 %fusion.12 = f32[256,8,64]{0,1,2:T(8,128)S(1)} fusion(f32[256,32,64]{0,2,1:T(8,128)S(1)} %subtract_bitcast_fusion, f32[256]{0:T(256)S(1)} %get-tuple-element.31, pred[128,8]{0,1:T(8,128)(4,1)S(1)} %get-tuple-element.34, s32[]{:T(128)S(6)} %select_n.3), kind=kOutput, calls=%fused_computation.14 | convolution fusion | flops 50462720 | bytes 2623492 | tf_op jit(solution)/shard_map/rtb,tk->rkb/dot_general | solution.py:89
  101.1 0.2 copy.38
  101.3 1.0 copy.43
  102.3 0.0 reduce-scatter.4.cloned.1.call-update
  103.6 0.2 multiply_reduce_fusion.1
  103.8 19.9 %reduce-scatter.4.cloned.1.call-done = f32[64,512]{1,0:T(8,128)} async-done(((f32[256,512]{1,0:T(8,128)}), f32[64,512]{1,0:T(8,128)}) %reduce-scatter.4.cloned.1.call-update) | async-done | bytes 131088
  123.7 1.0 copy.44
  124.7 0.7 convolution_bitcast_fusion.1
  125.5 5.8 %all-reduce.1 = (f32[8,8]{1,0:T(8,128)S(1)}, f32[8]{0:T(128)S(1)}) all-reduce(f32[8,8]{1,0:T(8,128)S(1)} %convolution_bitcast_fusion.1, f32[8]{0:T(128)S(1)} %multiply_reduce_fusion.1), channel_id=1, replica_groups=mesh['samp'=8,'snp'=4] {'snp'}, use_global_device_ids=true, to_apply=%region_10.0 | all-reduce | flops 72 | bytes 576 | tf_op jit(solution)/shard_map/psum | solution.py:97
  131.3 21.6 %psum.46 = f32[8,8]{1,0:T(8,128)S(1)} all-reduce(f32[8,8]{1,0:T(8,128)S(1)} %get-tuple-element.17), channel_id=1, replica_groups=mesh['samp'=8,'snp'=4] {'samp'}, use_global_device_ids=true, to_apply=%region_11.0 | all-reduce | flops 64 | bytes 512 | tf_op jit(solution)/shard_map/psum | solution.py:97
  152.9 1.2 broadcast_divide_fusion
  154.1 0.7 copy.41
  154.8 0.6 multiply_divide_fusion
  (10 shorter events, 0.1 us)
Async XLA Ops:
  7.2 3.3 %copy-start = (bf16[256,64]{0,1:T(8,128)(2,1)S(1)}, bf16[256,64]{0,1:T(8,128)(2,1)}, u32[]{:S(2)}) copy-start(bf16[256,64]{0,1:T(8,128)(2,1)} %param.7) | copy-start | bytes 98308
  7.2 87.2 %all-reduce.4.cloned.1.call-start = ((), (), s32[]{:S(2)}) async-start(), calls=%async_computation.1 | async-start | bytes 2097152 | tf_op jit(solution)/shard_map/psum | solution.py:71
  11.2 1.2 copy-start.1
  11.2 1.3 copy-start.2
  12.3 111.4 %reduce-scatter.4.cloned.1.call-start = ((), (), s32[]{:S(2)}) async-start(), calls=%async_computation.2 | async-start | bytes 655360
Sparse Core Ops, SparseCore 0:
  12.4 81.8 all-reduce.3
  102.4 21.2 reduce-scatter.3
